TPU v7x, 32 devices: a whole 2x2x4 slice. The times are simulated.
32 devices in a mesh: dp: 8 (over z, y), tp: 4 (over x, core).
Axes of the slice: x: 2, y: 2, z: 4, core: 2. Of those that a mesh axis runs over, the one named last changes fastest.
Arguments:
- node_lat: bfloat16 [16, 1885, 128], P('dp', None, 'tp')
- edge_lat: bfloat16 [16, 10910, 128], P('dp', None, 'tp')
- senders: int32 [10910], replicated
- receivers: int32 [10910], replicated
- grad_node: bfloat16 [16, 1885, 128], P('dp', None, 'tp')
- grad_edge: bfloat16 [16, 10910, 128], P('dp', None, 'tp')
- edge_w1: bfloat16 [2, 3, 128, 128], P(None, None, 'tp')
- edge_b1: float32 [2, 128], replicated
- edge_w2: bfloat16 [2, 128, 128], P(None, None, 'tp')
- edge_vec: float32 [2, 3, 128], P(None, None, 'tp')
- node_w1: bfloat16 [2, 2, 128, 128], P(None, None, 'tp')
- node_b1: float32 [2, 128], replicated
- node_w2: bfloat16 [2, 128, 128], P(None, None, 'tp')
- node_vec: float32 [2, 3, 128], P(None, None, 'tp')
Outputs:
- output 1: bfloat16 [16, 1885, 128], P('dp', None, 'tp')
- output 2: bfloat16 [16, 10910, 128], P('dp', None, 'tp')
- output 3: bfloat16 [16, 1885, 128], P('dp', None, 'tp')
- output 4: bfloat16 [16, 10910, 128], P('dp', None, 'tp')
- output 5: float32 [2, 3, 128, 128], P(None, None, 'tp')
- output 6: float32 [2, 128], replicated
- output 7: float32 [2, 128, 128], P(None, None, 'tp')
- output 8: float32 [2, 3, 128], P(None, None, 'tp')
- output 9: float32 [2, 2, 128, 128], P(None, None, 'tp')
- output 10: float32 [2, 128], replicated
- output 11: float32 [2, 128, 128], P(None, None, 'tp')
- output 12: float32 [2, 3, 128], P(None, None, 'tp')
All inputs are finite; a program needn't handle non-finite values.
Results may differ from a plain program's by a relative error of at most 0.0186387.
Values sent between devices are 32-bit elements.
A program may use at most 1 GiB of HBM per device.

v0:
```python
import jax
import jax.numpy as jnp
from jax import lax
from jax.experimental import pallas as pl
from jax.experimental.pallas import tpu as pltpu
from jax.sharding import PartitionSpec as P

LN_EPS = 1e-5
D = 128
T = 256
TN = 384
EC = 512
KS = 1408
BF = jnp.bfloat16
F32 = jnp.float32
I16 = jnp.int16
MESH = pl.DeviceIdType.MESH
VM = pl.BlockSpec(memory_space=pltpu.VMEM)
HB = pl.BlockSpec(memory_space=pl.ANY)
GROUP = 4
BOTH = (0, 1)
THREE = (0, 1, 2)
OTHERS = (1, 2, 3)
EDGE_IN, GRAD_IN, EDGE_OUT, GRAD_OUT = range(4)
SEND_ORDER = (2, 3, 1)
LROWS = 7 * (D // 4)
HEAD = 16
SLABS = 8


def dot(a, b):
    return jnp.dot(a, b, preferred_element_type=F32)


def dot_nt(a, b):
    return lax.dot_general(a, b, (((1,), (1,)), ((), ())), preferred_element_type=F32)


def mat(k, n=1):
    return slice(k * D, (k + n) * D)


def rows_of(d):
    q = D // 4
    return slice(d * q, (d + 1) * q)


def at(step, width):
    return pl.ds(pl.multiple_of(step * width, width), width)


def loop(stop, body, start=0):
    def step(j, carry):
        body(j)
        return carry

    lax.fori_loop(start, stop, step, 0)


def column_sum(val):
    return jnp.sum(val, axis=0, keepdims=True)


def flip(val):
    return jnp.swapaxes(val, 0, 1)


def stacked(parts):
    return jnp.concatenate(parts, axis=0)


def beside(parts):
    return jnp.concatenate(parts, axis=1)


def slot(d):
    return d - 1


def sigmoid(hidden):
    return 1.0 / (1.0 + jnp.exp(-hidden))


def fold(val):
    total = val[:, mat(0)]
    for start in range(D, val.shape[1], D):
        total = total + val[:, start:start + D]
    return total


def swap_halves(val):
    return stacked([val[rows_of(d)] for d in (1, 0, 3, 2)])


def gather(table, keys, iota):
    acc = None
    nodes = table.shape[1]
    one, zero = jnp.ones((), BF), jnp.zeros((), BF)
    for base in range(0, nodes, T):
        width = min(T, nodes - base)
        ids = iota[0:width, :]
        hot = beside([jnp.where(ids == (key - jnp.asarray(base, I16)), one, zero) for key in keys])
        part = dot(table[:, base:base + width], hot)
        acc = part if acc is None else acc + part
    return acc


def scatter(acc_ref, val, cols, lanes):
    nodes = acc_ref.shape[1]
    one, zero = jnp.ones((), BF), jnp.zeros((), BF)
    row = lanes[0:1, :]
    for base in range(0, nodes, T):
        width = min(T, nodes - base)
        hot = beside([jnp.where((row + jnp.asarray(base + s, I16)) == cols, one, zero) for s in range(0, width, D)])
        acc_ref[:, base:base + width] += dot(val, hot)


def mlp_tail(hidden, w2t, vec):
    act = (hidden * sigmoid(hidden)).astype(BF)
    out = dot(w2t, act) + vec[0]
    mean = column_sum(out) / D
    centered = out - mean
    var = column_sum(centered * centered) / D
    inv = lax.rsqrt(var + LN_EPS)
    normed = centered * inv
    message = (normed * vec[1] + vec[2]).astype(BF)
    return message, normed, inv


def mlp_back(d_msg, hidden, normed, inv, w2, vec):
    d_normed = d_msg * vec[1]
    mean0 = column_sum(d_normed) / D
    mean1 = column_sum(d_normed * normed) / D
    d_out = inv * (d_normed - mean0 - normed * mean1)
    d_out_bf = d_out.astype(BF)
    sig = sigmoid(hidden)
    act = (hidden * sig).astype(BF)
    d_w2 = dot_nt(d_out_bf, act)
    d_hidden = dot(w2, d_out_bf) * (sig * (1.0 + hidden * (1.0 - sig)))
    sums = (fold(d_out), fold(d_msg * normed), fold(d_msg), fold(d_hidden))
    return d_hidden.astype(BF), d_w2, sums


def add_sums(ref, parts):
    for q in range(4):
        total = parts[0][q]
        for other in parts[1:]:
            total = total + other[q]
        ref[mat(q), :] += total


def step_kernel(dims, *refs):
    layers, cols, nodes, edges, npad, eh, dpn = dims
    nch = eh // EC
    top = layers - 1
    n_in = 11
    (node_in, edge_in, gnode_in, gedge_in, idx, ew1_in, ew2_in, nw1_in, nw2_in, vec_in, b1_in) = refs[:n_in]
    n_out = 12
    (node_out, edge_out, dnode_out, dedge_out, ew1_out, eb1_out, ew2_out, evec_out, nw1_out, nb1_out, nw2_out, nvec_out) = refs[n_in:n_in + n_out]
    (node_raw, gnode_raw, edge_raw, gedge_raw, w_send, w_recv, n_send, n_recv, gn_send, gn_recv, no_send, no_recv, dn_send, dn_recv,
     e_send, g_send, e_recv, g_recv, eo_recv, de_recv, part, part_recv, hidden, normed, inv, nhid, nnrm, ninv, d_part, s_sum, r_sum,
     sums, grad, core_recv, half, dp_recv, cross_send, cross_recv, own_sum, gathered,
     core_ss, core_rs, dp_ss, dp_rs, cross_ss, cross_rs, load_sem, w_ss, w_rs, n_ss, n_rs, e_ss, e_rs, p_ss, p_rs, out_sem) = refs[n_in + n_out:]

    t = lax.axis_index('tp')
    p = lax.axis_index('dp')
    per = SLABS // dpn
    dp_others = range(1, dpn)
    x, c = t // 2, lax.rem(t, 2)
    ox, oc = 1 - x, 1 - c
    peer = [t, t + 1 - 2 * c, t + 2 - 4 * x, t + 3 - 2 * c - 4 * x]

    def remote(src, dst, ssem, rsem, d):
        return pltpu.make_async_remote_copy(src_ref=src, dst_ref=dst, send_sem=ssem, recv_sem=rsem,
                                            device_id={'tp': peer[d]}, device_id_type=MESH)

    loads = [pltpu.make_async_copy(src, dst, load_sem.at[q]) for q, (src, dst) in enumerate(
        [(node_in, node_raw), (edge_in, edge_raw), (gnode_in, gnode_raw), (gedge_in, gedge_raw)])]
    for copy in loads:
        copy.start()

    barrier = pltpu.get_barrier_semaphore()
    for d in OTHERS:
        pl.semaphore_signal(barrier, inc=1, device_id={'tp': peer[d]}, device_id_type=MESH)
    for i in dp_others:
        pl.semaphore_signal(barrier, inc=1, device_id={'dp': lax.rem(p + i, dpn)}, device_id_type=MESH)
    pl.semaphore_wait(barrier, len(OTHERS) + dpn - 1)

    def node_copies(send, recv, kind):
        return (remote(send.at[1], recv.at[0], n_ss.at[kind, 0], n_rs.at[kind, 0], 1),
                remote(send.at[0], recv.at[1], n_ss.at[kind, 1], n_rs.at[kind, 1], 2),
                remote(recv.at[1], recv.at[2], n_ss.at[kind, 2], n_rs.at[kind, 2], 1))

    def weight_copies(kind):
        rows = (pl.ds(0, HEAD + LROWS), pl.ds(HEAD + LROWS, LROWS * (top)))[kind]
        return (remote(w_send.at[rows], w_recv.at[0, rows], w_ss.at[kind, 0], w_rs.at[kind, 0], 1),
                remote(w_send.at[rows], w_recv.at[1, rows], w_ss.at[kind, 1], w_rs.at[kind, 1], 2),
                remote(w_recv.at[1, rows], w_recv.at[2, rows], w_ss.at[kind, 2], w_rs.at[kind, 2], 1))

    def edge_copy(kind, j, d):
        src, dst = ((e_send, e_recv), (g_send, g_recv), (e_send, eo_recv), (g_send, de_recv))[kind]
        lanes_j = at(j, EC)
        return remote(src.at[slot(d), :, lanes_j], dst.at[slot(d), :, lanes_j], e_ss.at[kind, slot(d), j], e_rs.at[kind, slot(d), j], d)

    def core_copy(l, b):
        return remote(grad.at[l, :, pl.ds((2 * b + 1) * cols, cols), :], core_recv.at[l, b], core_ss.at[l, b], core_rs.at[l, b], 1)

    def dp_remote(src, dst, stage, l, i):
        return pltpu.make_async_remote_copy(src_ref=src, dst_ref=dst, send_sem=dp_ss.at[stage, l, i - 1], recv_sem=dp_rs.at[stage, l, i - 1],
                                            device_id={'dp': lax.rem(p + i, dpn)}, device_id_type=MESH)

    def spread_copy(l, i):
        return dp_remote(half.at[l, pl.ds(lax.rem(p + i, dpn) * per, per)], dp_recv.at[l, i - 1], 0, l, i)

    def cross_copy(l):
        return remote(cross_send.at[l], cross_recv.at[l], cross_ss.at[l], cross_rs.at[l], 2)

    def gather_copy(l, i, owner):
        return dp_remote(own_sum.at[l], gathered.at[l, pl.ds(owner * per, per)], 1, l, i)

    def part_copy(q):
        return remote(part.at[q], part_recv.at[q], p_ss.at[q], p_rs.at[q], 1)

    def load_nodes(raw, send, own):
        send[...] = jnp.zeros_like(send)
        send[0, :, :nodes] = raw[ox].astype(F32)
        send[1, :, :nodes] = raw[x].astype(F32)
        own[:cols, :] = send[1].astype(own.dtype)

    def load_edges(raw, send, own, kind):
        def put(j, lanes_j, val_of):
            for d in OTHERS:
                sample = x if d < 2 else ox
                send[slot(d), :, lanes_j] = val_of(sample, oc if d % 2 else c).astype(F32)
            own[:cols, lanes_j] = val_of(x, c)

        def chunk(j):
            put(j, at(j, EC), lambda s, h: raw[s, :, pl.ds(pl.multiple_of(h * eh + j * EC, D), EC)])
            for d in SEND_ORDER:
                edge_copy(kind, j, d).start()

        loop(nch - 1, chunk)
        first = (nch - 1) * EC
        used = edges - eh - first
        last = pl.ds(first, EC)

        def tail(s, h):
            left = raw[s, :, pl.ds(first, EC)]
            right = beside([raw[s, :, pl.ds(eh + first, used)], jnp.zeros((cols, EC - used), BF)])
            return jnp.where(h == 0, left.astype(F32), right.astype(F32)).astype(BF)

        put(nch - 1, last, tail)
        for d in SEND_ORDER:
            edge_copy(kind, nch - 1, d).start()

    def place_edges(raw, block, d, j):
        s = x if d < 2 else ox
        h = oc if d % 2 else c
        val = block.astype(BF)
        first = (nch - 1) * EC
        used = edges - eh - first

        @pl.when(jnp.logical_or(j < nch - 1, h == 0))
        def _():
            raw[s, :, pl.ds(pl.multiple_of(h * eh + j * EC, D), EC)] = val

        @pl.when(jnp.logical_and(j == nch - 1, h == 1))
        def _():
            raw[s, :, pl.ds(eh + first, used)] = val[:, :used]

    def scoped(e0, e1, ge, msg, v0, v1, v2, agg0, agg1, d_agg, scol, rcol, srow, rrow, iota, lanes, ew1, ew1t, ew2, ew2t, nw1, nw1t, nw2, nw2t, vecs):
        tables = (v0, v1, v2)
        aggs = (agg0, agg1)
        edges_in = (e0, e1)

        loads[0].wait()
        load_nodes(node_raw, n_send, v0)
        ncop = node_copies(n_send, n_recv, 0)
        ncop[1].start()
        ncop[0].start()
        q = cols
        w_send[:HEAD, :cols] = vec_in[...]
        for l in range(layers):
            off = HEAD + l * LROWS
            w_send[off:off + 3 * q, :] = ew1_in[l * 3 * q:(l + 1) * 3 * q, :].astype(F32)
            w_send[off + 3 * q:off + 4 * q, :] = ew2_in[l * q:(l + 1) * q, :].astype(F32)
            w_send[off + 4 * q:off + 6 * q, :] = nw1_in[l * 2 * q:(l + 1) * 2 * q, :].astype(F32)
            w_send[off + 6 * q:off + 7 * q, :] = nw2_in[l * q:(l + 1) * q, :].astype(F32)
        wcop = [weight_copies(kind) for kind in range(2)]
        wcop[0][1].start()
        wcop[0][0].start()
        loads[1].wait()
        load_edges(edge_raw, e_send, e0, EDGE_IN)
        wcop[1][1].start()
        wcop[1][0].start()
        loads[2].wait()
        load_nodes(gnode_raw, gn_send, d_part)
        gcop = node_copies(gn_send, gn_recv, 1)
        gcop[1].start()
        gcop[0].start()
        loads[3].wait()
        load_edges(gedge_raw, g_send, ge, GRAD_IN)

        iota[...] = lax.broadcasted_iota(jnp.int32, (T, D), 0).astype(I16)
        lanes[...] = lax.broadcasted_iota(jnp.int32, (16, D), 1).astype(I16)

        def ids(b):
            for which, (row_ref, col_ref) in enumerate(((srow, scol), (rrow, rcol))):
                row = idx[which, pl.ds(c * (eh // D) + b, 1), :]
                wide = jnp.broadcast_to(row, (D, D))
                row_ref[at(b, 16), :] = wide[:16].astype(I16)
                col_ref[at(b, D), :] = flip(wide.astype(F32)).astype(jnp.int32).astype(I16)

        loop(eh // D, ids)

        def keys(ref, step):
            return [ref[pl.ds(pl.multiple_of(step * (T // D) * 16 + 16 * h, 16), 1), :] for h in range(T // D)]

        def join_weights(l):
            off = HEAD + l * LROWS
            for d in range(GROUP):
                src = w_send if d == 0 else w_recv.at[slot(d)]
                r = slice(d * q, (d + 1) * q)
                for k in THREE:
                    ew1[l, k * D + d * q:k * D + (d + 1) * q, :] = src[off + k * q:off + (k + 1) * q, :].astype(BF)
                ew2t[l, r, :] = src[off + 3 * q:off + 4 * q, :].astype(BF)
                for k in range(2):
                    nw1[l, k * D + d * q:k * D + (d + 1) * q, :] = src[off + (4 + k) * q:off + (5 + k) * q, :].astype(BF)
                nw2t[l, r, :] = src[off + 6 * q:off + 7 * q, :].astype(BF)

            def flip_bf(mat):
                return flip(mat.astype(F32)).astype(BF)

            for k in THREE:
                ew1t[l, :, mat(k)] = flip_bf(ew1[l, mat(k), :])
            for k in range(2):
                nw1t[l, :, mat(k)] = flip_bf(nw1[l, mat(k), :])
            ew2[l] = flip_bf(ew2t[l])
            nw2[l] = flip_bf(nw2t[l])

        def wait_recvs(copies):
            copies[1].wait_recv()
            copies[2].start()
            copies[0].wait_recv()
            copies[2].wait_recv()

        wait_recvs(ncop)
        for d in OTHERS:
            v0[rows_of(d), :] = n_recv[slot(d)].astype(BF)
        wait_recvs(wcop[0])
        rows_all = beside([w_send[:HEAD, :cols]] + [w_recv[d, :HEAD, :cols] for d in range(3)])
        vecs[...] = flip(stacked([rows_all, jnp.zeros((D - HEAD, D), F32)]))
        join_weights(0)

        def vec(l, node):
            first = 6 * node + l
            return [vecs[:, first + 2 * k:first + 2 * k + 1] for k in THREE]

        def bias(l, node):
            return b1_in[:, 2 * node + l:2 * node + l + 1]

        def hidden_of_nodes(l):
            table, b1 = tables[l], bias(l, 0)

            def body(step):
                xs = gather(table, keys(srow, step), iota).astype(BF)
                xr = gather(table, keys(rrow, step), iota).astype(BF)
                hidden[l, :, at(step, T)] = dot(ew1t[l, :, mat(1, 2)], stacked([xs, xr])) + b1

            loop(eh // T, body)

        def edge_forward(l):
            e_in = edges_in[l]

            def body(j):
                for sub in range(EC // T):
                    a = at(j * (EC // T) + sub, T)
                    if l == 0:
                        if sub == 0:
                            for d in OTHERS:
                                edge_copy(EDGE_IN, j, d).wait_recv()
                        for d in OTHERS:
                            e_in[rows_of(d), a] = e_recv[slot(d), :, a].astype(BF)
                    e_val = e_in[:, a]
                    hid = hidden[l, :, a] + dot(ew1t[l, :, mat(0)], e_val)
                    hidden[l, :, a] = hid
                    message, nrm, std = mlp_tail(hid, ew2t[l], vec(l, 0))
                    normed[l, :, a] = nrm
                    inv[l:l + 1, a] = std
                    msg[:, a] = message
                    e_new = (e_val.astype(F32) + message.astype(F32)).astype(BF)
                    if l < top:
                        edges_in[l + 1][:, a] = e_new
                    else:
                        for d in OTHERS:
                            e_send[slot(d), :, a] = e_new[rows_of(d)].astype(F32)
                        if sub == 0:
                            own_parts = []
                        own_parts.append(e_new[:q])
                if l == top:
                    for d in SEND_ORDER:
                        edge_copy(EDGE_OUT, j, d).start()
                    place_edges(edge_raw, beside(own_parts), 0, j)

            loop(nch, body)

        def segment_sum(acc, ids_ref):
            acc[...] = jnp.zeros(acc.shape, F32)

            def body(step):
                scatter(acc, msg[:, at(step, KS)], ids_ref[at(step, KS), :], lanes)

            loop(eh // KS, body)

        def node_forward(l):
            table, agg, out = tables[l], aggs[l], tables[l + 1]

            def body(step):
                a = pl.ds(pl.multiple_of(step * TN, D), TN)
                v_in = table[:, a]
                agg_bf = (part[l, :, a] + swap_halves(part_recv[l, :, a])).astype(BF)
                agg[:, a] = agg_bf
                hid = dot(nw1t[l], stacked([v_in, agg_bf])) + bias(l, 1)
                nhid[l, :, a] = hid
                message, nrm, std = mlp_tail(hid, nw2t[l], vec(l, 1))
                nnrm[l, :, a] = nrm
                ninv[l:l + 1, a] = std
                out[:, a] = (v_in.astype(F32) + message.astype(F32)).astype(BF)

            loop(npad // TN, body)

        for l in range(layers):
            hidden_of_nodes(l)
            if l == top:
                def drain(j):
                    for d in OTHERS:
                        edge_copy(EDGE_IN, j, d).wait_send()
                loop(nch, drain)
            edge_forward(l)
            segment_sum(part.at[l], rcol)
            part_copy(l).start()
            if l == 0:
                wait_recvs(wcop[1])
                join_weights(1)
            part_copy(l).wait_recv()
            node_forward(l)
        no_send[...] = tables[layers][2 * q:3 * q, :].astype(F32)
        no_copy = remote(no_send, no_recv, n_ss.at[2, 0], n_rs.at[2, 0], 2)
        no_copy.start()
        node_raw[x] = tables[layers][:q, :nodes]

        hold = nch // 2
        grad[...] = jnp.zeros_like(grad)
        sums[...] = jnp.zeros_like(sums)
        wait_recvs(gcop)
        for d in OTHERS:
            d_part[rows_of(d), :] = gn_recv[slot(d)]

        def node_backward(l):
            table, agg = tables[l], aggs[l]

            def body(step):
                a = pl.ds(pl.multiple_of(step * TN, D), TN)
                d_in = d_part[:, a]
                if l < top:
                    d_in = d_in + part[layers + l + 1, :, a] + swap_halves(part_recv[layers + l + 1, :, a])
                    d_in = d_in.astype(BF).astype(F32)
                d_hid, d_w2, parts = mlp_back(d_in, nhid[l, :, a], nnrm[l, :, a], ninv[l:l + 1, a], nw2[l], vec(l, 1))
                add_sums(sums.at[l, 1], [parts])
                grad[l, 6] += d_w2
                grad[l, 4] += dot_nt(table[:, a], d_hid)
                grad[l, 5] += dot_nt(agg[:, a], d_hid)
                d_part[:, a] = d_in + dot(nw1[l, mat(0), :], d_hid)
                d_agg[:, a] = dot(nw1[l, mat(1), :], d_hid).astype(BF)

            loop(npad // TN, body)

        def gather_back():
            def body(step):
                msg[:, at(step, T)] = gather(d_agg, keys(rrow, step), iota).astype(BF)

            loop(eh // T, body)

        def edge_backward(l):
            e_in = edges_in[l]

            def body(j):
                all_parts, d_w2s, d_w1s, own_parts = [], [], [], []
                for sub in range(EC // T):
                    a = at(j * (EC // T) + sub, T)
                    if l == top:
                        if sub == 0:
                            for d in OTHERS:
                                edge_copy(GRAD_IN, j, d).wait_recv()
                        for d in OTHERS:
                            ge[rows_of(d), a] = g_recv[slot(d), :, a].astype(BF)
                    d_res = ge[:, a].astype(F32)
                    d_msg = d_res + msg[:, a].astype(F32)
                    d_hid, d_w2, parts = mlp_back(d_msg, hidden[l, :, a], normed[l, :, a], inv[l:l + 1, a], ew2[l], vec(l, 0))
                    all_parts.append(parts)
                    d_w2s.append(d_w2)
                    d_w1s.append(dot_nt(e_in[:, a], d_hid))
                    msg[:, a] = d_hid
                    d_new = (d_res + dot(ew1[l, mat(0), :], d_hid)).astype(BF)
                    if l > 0:
                        ge[:, a] = d_new
                    else:
                        for d in OTHERS:
                            g_send[slot(d), :, a] = d_new[rows_of(d)].astype(F32)
                        own_parts.append(d_new[:q])
                add_sums(sums.at[l, 0], all_parts)
                grad[l, 3] += sum(d_w2s[1:], d_w2s[0])
                grad[l, 0] += sum(d_w1s[1:], d_w1s[0])
                if l == 0:
                    @pl.when(j < hold)
                    def _():
                        for d in SEND_ORDER:
                            edge_copy(GRAD_OUT, j, d).start()
                    place_edges(gedge_raw, beside(own_parts), 0, j)

            loop(nch, body)

        def reduce_start(l):
            def total(node, k):
                return column_sum(flip(sums[l, node, mat(k), :]))

            lat = stacked([total(node, k) for node in BOTH for k in THREE])
            biases = stacked([total(node, 3) for node in BOTH])
            n_lat = lat.shape[0]
            for d in range(GROUP):
                grad[l, SLABS - 1, d * cols:d * cols + n_lat, :cols] = lat[:, rows_of(d)]
                grad[l, SLABS - 1, d * cols + n_lat:d * cols + n_lat + 2, :] = biases
            for b in BOTH:
                core_copy(l, b).start()

        def chip_sum(l):
            row = lax.broadcasted_iota(jnp.int32, (cols, D), 0)
            edge_row = jnp.logical_or(row < 3, row == 6)
            for b in BOTH:
                core_copy(l, b).wait_recv()
                for k in range(SLABS):
                    own = grad[l, k, rows_of(2 * b), :]
                    if k < 4:
                        own = own + core_recv[l, b, k]
                    elif k == SLABS - 1:
                        own = own + jnp.where(edge_row, core_recv[l, b, k], 0.0)
                    half[l, k, b] = own
            for i in dp_others:
                spread_copy(l, i).start()

        def dp_sum(l):
            total = half[l, pl.ds(p * per, per)]
            for i in dp_others:
                spread_copy(l, i).wait_recv()
                total = total + dp_recv[l, i - 1]
            own_sum[l] = total[:, 0]
            cross_send[l] = total[:, 1]
            cross_copy(l).start()

        def cross_sum(l):
            cross_copy(l).wait_recv()
            total = own_sum[l] + cross_recv[l]
            own_sum[l] = total
            gathered[l, pl.ds(p * per, per)] = total
            for i in dp_others:
                gather_copy(l, i, p).start()

        def project(l):
            table = tables[l]

            def body(step):
                a = pl.ds(pl.multiple_of(step * TN, D), TN)
                s_bf, r_bf, v_in = s_sum[:, a].astype(BF), r_sum[:, a].astype(BF), table[:, a]
                part[layers + l, :, a] = dot(ew1[l, mat(1), :], s_bf) + dot(ew1[l, mat(2), :], r_bf)
                grad[l, 1] += dot_nt(v_in, s_bf)
                grad[l, 2] += dot_nt(v_in, r_bf)

            loop(npad // TN, body)

        for l in reversed(range(layers)):
            node_backward(l)
            if l < top:
                chip_sum(l + 1)
            gather_back()
            if l == 0:
                def drain_g(j):
                    for d in OTHERS:
                        edge_copy(GRAD_IN, j, d).wait_send()
                loop(nch, drain_g)
            edge_backward(l)
            if l < top:
                dp_sum(l + 1)
            segment_sum(s_sum, scol)
            segment_sum(r_sum, rcol)
            project(l)
            part_copy(layers + l).start()
            reduce_start(l)
            part_copy(layers + l).wait_recv()

        def final(step):
            a = pl.ds(pl.multiple_of(step * TN, D), TN)
            d_in = (d_part[:, a] + part[layers, :, a] + swap_halves(part_recv[layers, :, a])).astype(BF)
            v2[:, a] = d_in

        loop(npad // TN, final)
        dn_send[...] = v2[2 * q:3 * q, :].astype(F32)
        dn_copy = remote(dn_send, dn_recv, n_ss.at[2, 1], n_rs.at[2, 1], 2)
        dn_copy.start()
        gnode_raw[x] = v2[:q, :nodes]
        chip_sum(0)

        no_copy.wait_recv()
        node_raw[ox] = no_recv[:, :nodes].astype(BF)

        def place_e(j):
            for d in OTHERS:
                edge_copy(EDGE_OUT, j, d).wait_recv()
                place_edges(edge_raw, eo_recv[slot(d), :, at(j, EC)], d, j)

        loop(nch, place_e)
        outs = [pltpu.make_async_copy(src, dst, out_sem.at[k]) for k, (src, dst) in enumerate(
            [(node_raw, node_out), (edge_raw, edge_out), (gnode_raw, dnode_out), (gedge_raw, dedge_out)])]
        outs[0].start()
        outs[1].start()

        dp_sum(0)

        def send_rest(j):
            for d in SEND_ORDER:
                edge_copy(GRAD_OUT, j, d).start()

        loop(nch, send_rest, hold)

        def place_g(j):
            for d in OTHERS:
                edge_copy(GRAD_OUT, j, d).wait_recv()
                place_edges(gedge_raw, de_recv[slot(d), :, at(j, EC)], d, j)

        loop(hold, place_g)
        for l in range(layers):
            cross_sum(l)
        loop(nch, place_g, hold)
        outs[3].start()
        dn_copy.wait_recv()
        gnode_raw[ox] = dn_recv[:, :nodes].astype(BF)
        outs[2].start()

        for l in range(layers):
            for i in dp_others:
                gather_copy(l, i, lax.rem(p + dpn - i, dpn)).wait_recv()
            ew1_out[l] = gathered[l, 0:3]
            ew2_out[l] = gathered[l, 3]
            nw1_out[l] = gathered[l, 4:6]
            nw2_out[l] = gathered[l, 6]
            small = gathered[l, SLABS - 1]
            for k in THREE:
                evec_out[k, l:l + 1, :] = small[k:k + 1, :cols]
                nvec_out[k, l:l + 1, :] = small[3 + k:4 + k, :cols]
            eb1_out[l:l + 1, :] = small[6:7]
            nb1_out[l:l + 1, :] = small[7:8]

        for l in range(layers):
            for b in BOTH:
                core_copy(l, b).wait_send()
            cross_copy(l).wait_send()
            for i in dp_others:
                spread_copy(l, i).wait_send()
                gather_copy(l, i, p).wait_send()
        for copies in (ncop, gcop, wcop[0], wcop[1]):
            for copy in copies:
                copy.wait_send()
        no_copy.wait_send()
        dn_copy.wait_send()
        for k in range(2 * layers):
            part_copy(k).wait_send()

        def drain_out(j):
            for kind in (EDGE_OUT, GRAD_OUT):
                for d in OTHERS:
                    edge_copy(kind, j, d).wait_send()

        loop(nch, drain_out)
        for copy in outs:
            copy.wait()

    bf = lambda *s: pltpu.VMEM(s, BF)
    pl.run_scoped(
        scoped, bf(D, eh), bf(D, eh), bf(D, eh), bf(D, eh), bf(D, npad), bf(D, npad), bf(D, npad), bf(D, npad), bf(D, npad), bf(D, npad),
        pltpu.VMEM((eh, D), I16), pltpu.VMEM((eh, D), I16), pltpu.VMEM((eh // D * 16, D), I16), pltpu.VMEM((eh // D * 16, D), I16),
        pltpu.VMEM((T, D), I16), pltpu.VMEM((16, D), I16),
        bf(layers, 3 * D, D), bf(layers, D, 3 * D), bf(layers, D, D), bf(layers, D, D),
        bf(layers, 2 * D, D), bf(layers, D, 2 * D), bf(layers, D, D), bf(layers, D, D), pltpu.VMEM((D, D), F32))


def solution(mesh):
    lat_spec = P('dp', None, 'tp')
    first_spec = P(None, None, 'tp', None)
    col_spec = P(None, None, 'tp')
    param_specs = (first_spec, P(), col_spec, col_spec, first_spec, P(), col_spec, col_spec)
    in_specs = (lat_spec, lat_spec, P(), P(), lat_spec, lat_spec) + param_specs
    out_specs = (lat_spec, lat_spec, lat_spec, lat_spec) + param_specs
    shape = jax.ShapeDtypeStruct

    def local_step(node_lat, edge_lat, senders, receivers, grad_node, grad_edge, edge_w1, edge_b1, edge_w2, edge_vec, node_w1, node_b1, node_w2, node_vec):
        layers = edge_w1.shape[0]
        cols = node_lat.shape[2]
        nodes, edges = node_lat.shape[1], edge_lat.shape[1]
        npad = -(-nodes // TN) * TN
        eh = -(-edges // (2 * EC)) * EC
        nch = eh // EC
        dpn = mesh.shape['dp']
        per = SLABS // dpn
        dims = (layers, cols, nodes, edges, npad, eh, dpn)
        flat = lambda arr: jnp.swapaxes(arr, 1, 2)
        idx = jnp.pad(jnp.stack([senders, receivers]), ((0, 0), (0, 2 * eh - edges)), constant_values=-1).reshape(2, 2 * eh // D, D)
        vec_in = jnp.concatenate([jnp.transpose(edge_vec, (1, 0, 2)).reshape(-1, cols), jnp.transpose(node_vec, (1, 0, 2)).reshape(-1, cols),
                                  jnp.zeros((HEAD - 6 * layers, cols), F32)], axis=0)
        b1_in = jnp.transpose(stacked([edge_b1, node_b1]))
        args = (flat(node_lat), flat(edge_lat), flat(grad_node), flat(grad_edge), idx,
                edge_w1.reshape(-1, D), flat(edge_w2).reshape(-1, D), node_w1.reshape(-1, D), flat(node_w2).reshape(-1, D), vec_in, b1_in)
        vm, sem = pltpu.VMEM, pltpu.SemaphoreType.DMA
        wrows = HEAD + layers * LROWS
        lat_n, lat_e = (2, cols, nodes), (2, cols, edges)
        scratch = [
            vm(lat_n, BF), vm(lat_n, BF), vm(lat_e, BF), vm(lat_e, BF), vm((wrows, D), F32), vm((3, wrows, D), F32),
            vm((2, cols, npad), F32), vm((3, cols, npad), F32), vm((2, cols, npad), F32), vm((3, cols, npad), F32),
            vm((cols, npad), F32), vm((cols, npad), F32), vm((cols, npad), F32), vm((cols, npad), F32),
            vm((3, cols, eh), F32), vm((3, cols, eh), F32), vm((3, cols, eh), F32), vm((3, cols, eh), F32), vm((3, cols, eh), F32), vm((3, cols, eh), F32),
            vm((2 * layers, D, npad), F32), vm((2 * layers, D, npad), F32),
            vm((layers, D, eh), F32), vm((layers, D, eh), F32), vm((8, eh), F32),
            vm((layers, D, npad), F32), vm((layers, D, npad), F32), vm((8, npad), F32),
            vm((D, npad), F32), vm((D, npad), F32), vm((D, npad), F32), vm((layers, 2, 4 * D, D), F32),
            vm((layers, SLABS, D, D), F32), vm((layers, 2, SLABS, cols, D), F32), vm((layers, SLABS, 2, cols, D), F32),
            vm((layers, dpn - 1, per, 2, cols, D), F32), vm((layers, per, cols, D), F32), vm((layers, per, cols, D), F32),
            vm((layers, per, cols, D), F32), vm((layers, SLABS, cols, D), F32),
            sem((layers, 2)), sem((layers, 2)), sem((2, layers, dpn - 1)), sem((2, layers, dpn - 1)), sem((layers,)), sem((layers,)),
            sem((4,)), sem((2, 3)), sem((2, 3)), sem((3, 3)), sem((3, 3)), sem((4, 3, nch)), sem((4, 3, nch)),
            sem((2 * layers,)), sem((2 * layers,)), sem((4,))]
        outs = [shape(lat_n, BF), shape(lat_e, BF), shape(lat_n, BF), shape(lat_e, BF),
                shape((layers, 3, cols, D), F32), shape((layers, D), F32), shape((layers, cols, D), F32), shape((3, layers, cols), F32),
                shape((layers, 2, cols, D), F32), shape((layers, D), F32), shape((layers, cols, D), F32), shape((3, layers, cols), F32)]
        res = pl.pallas_call(
            lambda *refs: step_kernel(dims, *refs),
            name='graph_step',
            out_shape=outs,
            in_specs=[HB] * 4 + [VM] * 7,
            out_specs=[HB] * 4 + [VM] * 8,
            scratch_shapes=scratch,
            compiler_params=pltpu.CompilerParams(collective_id=0, has_side_effects=True, vmem_limit_bytes=67_043_328),
        )(*args)

        lead = lambda arr: jnp.transpose(arr, (1, 0, 2))
        return (flat(res[0]), flat(res[1]), flat(res[2]), flat(res[3]),
                res[4], res[5], flat(res[6]), lead(res[7]), res[8], res[9], flat(res[10]), lead(res[11]))

    return jax.shard_map(local_step, mesh=mesh, in_specs=in_specs, out_specs=out_specs, check_vma=False)
```

profile of v0, /device:TPU:0, one launch (start us, length us, event | category | flops | bytes accessed | tf_op | source)
XLA Modules:
  0.0 195.0 jit_solution(9370027686637443535)
XLA Ops:
  0.7 0.1 pad.9.clone
  0.7 0.7 pad_maximum_fusion
  1.4 0.7 reshape.50
  2.1 0.7 reshape.51
  2.8 0.7 maximum_maximum_fusion.refs_9_
  3.5 0.8 stack.9
  4.3 0.8 stack.10
  5.1 0.1 pad_add_fusion
  5.3 0.6 copy.31
  5.9 0.7 copy.28
  6.6 177.4 %graph_step.1 = (bf16[2,32,1885]{2,1,0:T(8,128)(2,1)}, bf16[2,32,10910]{2,1,0:T(8,128)(2,1)}, bf16[2,32,1885]{2,1,0:T(8,128)(2,1)}, bf16[2,32,10910]{2,1,0:T(8,1...) custom-call(bf16[2,32,1885]{2,1,0:T(8,128)(2,1)} %bitcast.34, ...), custom_call_target="tpu_custom_call" | custom-call | tf_op jit(solution)/shard_map/graph_step/pallas_call | solution.py:742
  184.1 1.7 copy.44
  185.7 2.7 %copy.45 = bf16[2,10910,32]{1,2,0:T(8,128)(2,1)} copy(bf16[2,10910,32]{1,2,0:T(8,128)(2,1)} %bitcast.31) | data formatting | bytes 2792960
  188.4 0.7 copy.46
  189.1 0.0 copy-done
  189.1 1.1 copy.47
  190.2 0.6 copy.48
  190.9 0.6 copy.49
  191.4 0.6 copy.50
  192.1 0.6 copy.51
  192.6 0.6 copy.52
  193.3 0.6 copy.53
  193.8 0.6 copy.54
  194.5 0.6 copy.55
  (21 shorter events, 0.1 us)
Async XLA Ops:
  185.7 2.7 %copy-start.1 = (bf16[2,32,1885]{2,1,0:T(8,128)(2,1)S(1)}, bf16[2,32,1885]{2,1,0:T(8,128)(2,1)}, u32[]{:S(2)}) copy-start(bf16[2,32,1885]{2,1,0:T(8,128)(2,1)} %get-tuple-element.26) | copy-start | bytes 723844
  185.7 3.4 %copy-start = (bf16[2,32,10910]{2,1,0:T(8,128)(2,1)S(1)}, bf16[2,32,10910]{2,1,0:T(8,128)(2,1)}, u32[]{:S(2)}) copy-start(bf16[2,32,10910]{2,1,0:T(8,128)(2,1)} %get-tuple-element.27) | copy-start | bytes 4189444
  189.1 1.2 copy-start.2
  189.1 1.8 copy-start.9
  189.1 2.4 %copy-start.5 = (f32[2,32,128]{2,1,0:T(8,128)S(1)}, f32[2,32,128]{2,1,0:T(8,128)}, u32[]{:S(2)}) copy-start(f32[2,32,128]{2,1,0:T(8,128)} %get-tuple-element.30) | copy-start | bytes 98308
  189.1 3.0 %copy-start.7 = (f32[3,2,32]{2,1,0:T(2,128)S(1)}, f32[3,2,32]{2,1,0:T(2,128)}, u32[]{:S(2)}) copy-start(f32[3,2,32]{2,1,0:T(2,128)} %get-tuple-element.31) | copy-start | bytes 2308
  189.1 3.5 %copy-start.3 = (f32[2,2,32,128]{3,2,1,0:T(8,128)S(1)}, f32[2,2,32,128]{3,2,1,0:T(8,128)}, u32[]{:S(2)}) copy-start(f32[2,2,32,128]{3,2,1,0:T(8,128)} %get-tuple-element.56) | copy-start | bytes 196612
  189.1 4.2 %copy-start.8 = (f32[2,128]{1,0:T(2,128)S(1)}, f32[2,128]{1,0:T(2,128)}, u32[]{:S(2)}) copy-start(f32[2,128]{1,0:T(2,128)} %get-tuple-element.57) | copy-start | bytes 3076
  189.1 4.7 %copy-start.4 = (f32[2,32,128]{2,1,0:T(8,128)S(1)}, f32[2,32,128]{2,1,0:T(8,128)}, u32[]{:S(2)}) copy-start(f32[2,32,128]{2,1,0:T(8,128)} %get-tuple-element.34) | copy-start | bytes 98308
  189.1 5.3 %copy-start.6 = (f32[3,2,32]{2,1,0:T(2,128)S(1)}, f32[3,2,32]{2,1,0:T(2,128)}, u32[]{:S(2)}) copy-start(f32[3,2,32]{2,1,0:T(2,128)} %get-tuple-element.35) | copy-start | bytes 2308
where the time goes:
time: 196 us; the launch traced here: 195 us
  Pallas kernels  177 us (90%)
  local copies, waits for them, and re-layouts  15.4 us (8%)
    pallas_call x1, Pallas kernels, local_step(): pl.pallas_call(lambda *refs: step_kernel(dims, *refs), name='graph_step',...  177 us
    unnamed x34, local copies, waits for them, and re-layouts  11.6 us

commit v1 on v0

--- a/solution.py
+++ b/solution.py
@@ -153,13 +153,13 @@
     layers, cols, nodes, edges, npad, eh, dpn = dims
     nch = eh // EC
     top = layers - 1
-    n_in = 11
-    (node_in, edge_in, gnode_in, gedge_in, idx, ew1_in, ew2_in, nw1_in, nw2_in, vec_in, b1_in) = refs[:n_in]
+    n_in = 14
+    (node_in, edge_in, gnode_in, gedge_in, send_ids, recv_ids, ew1_in, ew2_in, nw1_in, nw2_in, evec_in, nvec_in, eb1_in, nb1_in) = refs[:n_in]
     n_out = 12
     (node_out, edge_out, dnode_out, dedge_out, ew1_out, eb1_out, ew2_out, evec_out, nw1_out, nb1_out, nw2_out, nvec_out) = refs[n_in:n_in + n_out]
     (node_raw, gnode_raw, edge_raw, gedge_raw, w_send, w_recv, n_send, n_recv, gn_send, gn_recv, no_send, no_recv, dn_send, dn_recv,
      e_send, g_send, e_recv, g_recv, eo_recv, de_recv, part, part_recv, hidden, normed, inv, nhid, nnrm, ninv, d_part, s_sum, r_sum,
-     sums, grad, core_recv, half, dp_recv, cross_send, cross_recv, own_sum, gathered,
+     ids_raw, bias_cols, sums, grad, core_recv, half, dp_recv, cross_send, cross_recv, own_sum, gathered,
      core_ss, core_rs, dp_ss, dp_rs, cross_ss, cross_rs, load_sem, w_ss, w_rs, n_ss, n_rs, e_ss, e_rs, p_ss, p_rs, out_sem) = refs[n_in + n_out:]
 
     t = lax.axis_index('tp')
@@ -184,7 +184,8 @@
         pl.semaphore_signal(barrier, inc=1, device_id={'tp': peer[d]}, device_id_type=MESH)
     for i in dp_others:
         pl.semaphore_signal(barrier, inc=1, device_id={'dp': lax.rem(p + i, dpn)}, device_id_type=MESH)
-    pl.semaphore_wait(barrier, len(OTHERS) + dpn - 1)
+    with jax.named_scope('barrier'):
+        pl.semaphore_wait(barrier, len(OTHERS) + dpn - 1)
 
     def node_copies(send, recv, kind):
         return (remote(send.at[1], recv.at[0], n_ss.at[kind, 0], n_rs.at[kind, 0], 1),
@@ -274,12 +275,16 @@
         edges_in = (e0, e1)
 
         loads[0].wait()
-        load_nodes(node_raw, n_send, v0)
+        with jax.named_scope('send_nodes'):
+            load_nodes(node_raw, n_send, v0)
         ncop = node_copies(n_send, n_recv, 0)
         ncop[1].start()
         ncop[0].start()
         q = cols
-        w_send[:HEAD, :cols] = vec_in[...]
+        w_send[:HEAD, :] = jnp.zeros((HEAD, D), F32)
+        for k in THREE:
+            w_send[k * layers:(k + 1) * layers, :cols] = evec_in[k]
+            w_send[(3 + k) * layers:(4 + k) * layers, :cols] = nvec_in[k]
         for l in range(layers):
             off = HEAD + l * LROWS
             w_send[off:off + 3 * q, :] = ew1_in[l * 3 * q:(l + 1) * 3 * q, :].astype(F32)
@@ -290,7 +295,8 @@
         wcop[0][1].start()
         wcop[0][0].start()
         loads[1].wait()
-        load_edges(edge_raw, e_send, e0, EDGE_IN)
+        with jax.named_scope('send_edges'):
+            load_edges(edge_raw, e_send, e0, EDGE_IN)
         wcop[1][1].start()
         wcop[1][0].start()
         loads[2].wait()
@@ -299,22 +305,29 @@
         gcop[1].start()
         gcop[0].start()
         loads[3].wait()
-        load_edges(gedge_raw, g_send, ge, GRAD_IN)
+        with jax.named_scope('send_grads'):
+            load_edges(gedge_raw, g_send, ge, GRAD_IN)
 
         iota[...] = lax.broadcasted_iota(jnp.int32, (T, D), 0).astype(I16)
         lanes[...] = lax.broadcasted_iota(jnp.int32, (16, D), 1).astype(I16)
 
+        ids_raw[...] = jnp.full(ids_raw.shape, -1, jnp.int32)
+        for which, src in enumerate((send_ids, recv_ids)):
+            ids_raw[which:which + 1, :edges] = src[...].reshape(1, edges)
+
         def ids(b):
             for which, (row_ref, col_ref) in enumerate(((srow, scol), (rrow, rcol))):
-                row = idx[which, pl.ds(c * (eh // D) + b, 1), :]
-                wide = jnp.broadcast_to(row, (D, D))
+                wide = jnp.broadcast_to(ids_raw[which:which + 1, pl.ds(pl.multiple_of(c * eh + b * D, D), D)], (D, D))
                 row_ref[at(b, 16), :] = wide[:16].astype(I16)
                 col_ref[at(b, D), :] = flip(wide.astype(F32)).astype(jnp.int32).astype(I16)
 
-        loop(eh // D, ids)
+        with jax.named_scope('ids'):
+            loop(eh // D, ids)
 
         def keys(ref, step):
             return [ref[pl.ds(pl.multiple_of(step * (T // D) * 16 + 16 * h, 16), 1), :] for h in range(T // D)]
+
+        bias_cols[...] = flip(stacked([eb1_in[...], nb1_in[...], jnp.zeros((D - 2 * layers, D), F32)]))
 
         def join_weights(l):
             off = HEAD + l * LROWS
@@ -344,10 +357,12 @@
             copies[0].wait_recv()
             copies[2].wait_recv()
 
-        wait_recvs(ncop)
+        with jax.named_scope('node_wait'):
+            wait_recvs(ncop)
         for d in OTHERS:
             v0[rows_of(d), :] = n_recv[slot(d)].astype(BF)
-        wait_recvs(wcop[0])
+        with jax.named_scope('weight_wait'):
+            wait_recvs(wcop[0])
         rows_all = beside([w_send[:HEAD, :cols]] + [w_recv[d, :HEAD, :cols] for d in range(3)])
         vecs[...] = flip(stacked([rows_all, jnp.zeros((D - HEAD, D), F32)]))
         join_weights(0)
@@ -357,7 +372,7 @@
             return [vecs[:, first + 2 * k:first + 2 * k + 1] for k in THREE]
 
         def bias(l, node):
-            return b1_in[:, 2 * node + l:2 * node + l + 1]
+            return bias_cols[:, node * layers + l:node * layers + l + 1]
 
         def hidden_of_nodes(l):
             table, b1 = tables[l], bias(l, 0)
@@ -430,20 +445,25 @@
             loop(npad // TN, body)
 
         for l in range(layers):
-            hidden_of_nodes(l)
+            with jax.named_scope(f'gather_{l}'):
+                hidden_of_nodes(l)
             if l == top:
                 def drain(j):
                     for d in OTHERS:
                         edge_copy(EDGE_IN, j, d).wait_send()
                 loop(nch, drain)
-            edge_forward(l)
-            segment_sum(part.at[l], rcol)
+            with jax.named_scope(f'edge_forward_{l}'):
+                edge_forward(l)
+            with jax.named_scope(f'sum_{l}'):
+                segment_sum(part.at[l], rcol)
             part_copy(l).start()
             if l == 0:
                 wait_recvs(wcop[1])
                 join_weights(1)
-            part_copy(l).wait_recv()
-            node_forward(l)
+            with jax.named_scope(f'part_wait_{l}'):
+                part_copy(l).wait_recv()
+            with jax.named_scope(f'node_forward_{l}'):
+                node_forward(l)
         no_send[...] = tables[layers][2 * q:3 * q, :].astype(F32)
         no_copy = remote(no_send, no_recv, n_ss.at[2, 0], n_rs.at[2, 0], 2)
         no_copy.start()
@@ -452,7 +472,8 @@
         hold = nch // 2
         grad[...] = jnp.zeros_like(grad)
         sums[...] = jnp.zeros_like(sums)
-        wait_recvs(gcop)
+        with jax.named_scope('grad_node_wait'):
+            wait_recvs(gcop)
         for d in OTHERS:
             d_part[rows_of(d), :] = gn_recv[slot(d)]
 
@@ -578,24 +599,34 @@
             loop(npad // TN, body)
 
         for l in reversed(range(layers)):
-            node_backward(l)
+            with jax.named_scope(f'node_backward_{l}'):
+                node_backward(l)
             if l < top:
-                chip_sum(l + 1)
-            gather_back()
+                with jax.named_scope('chip_sum_1'):
+                    chip_sum(l + 1)
+            with jax.named_scope(f'gather_back_{l}'):
+                gather_back()
             if l == 0:
                 def drain_g(j):
                     for d in OTHERS:
                         edge_copy(GRAD_IN, j, d).wait_send()
                 loop(nch, drain_g)
-            edge_backward(l)
+            with jax.named_scope(f'edge_backward_{l}'):
+                edge_backward(l)
             if l < top:
-                dp_sum(l + 1)
-            segment_sum(s_sum, scol)
-            segment_sum(r_sum, rcol)
-            project(l)
+                with jax.named_scope('dp_sum_1'):
+                    dp_sum(l + 1)
+            with jax.named_scope(f'sum_send_{l}'):
+                segment_sum(s_sum, scol)
+            with jax.named_scope(f'sum_recv_{l}'):
+                segment_sum(r_sum, rcol)
+            with jax.named_scope(f'project_{l}'):
+                project(l)
             part_copy(layers + l).start()
-            reduce_start(l)
-            part_copy(layers + l).wait_recv()
+            with jax.named_scope(f'reduce_start_{l}'):
+                reduce_start(l)
+            with jax.named_scope(f'back_wait_{l}'):
+                part_copy(layers + l).wait_recv()
 
         def final(step):
             a = pl.ds(pl.multiple_of(step * TN, D), TN)
@@ -607,9 +638,11 @@
         dn_copy = remote(dn_send, dn_recv, n_ss.at[2, 1], n_rs.at[2, 1], 2)
         dn_copy.start()
         gnode_raw[x] = v2[:q, :nodes]
-        chip_sum(0)
-
-        no_copy.wait_recv()
+        with jax.named_scope('chip_sum_0'):
+            chip_sum(0)
+
+        with jax.named_scope('node_out_wait'):
+            no_copy.wait_recv()
         node_raw[ox] = no_recv[:, :nodes].astype(BF)
 
         def place_e(j):
@@ -617,13 +650,15 @@
                 edge_copy(EDGE_OUT, j, d).wait_recv()
                 place_edges(edge_raw, eo_recv[slot(d), :, at(j, EC)], d, j)
 
-        loop(nch, place_e)
+        with jax.named_scope('place_edge_out'):
+            loop(nch, place_e)
         outs = [pltpu.make_async_copy(src, dst, out_sem.at[k]) for k, (src, dst) in enumerate(
             [(node_raw, node_out), (edge_raw, edge_out), (gnode_raw, dnode_out), (gedge_raw, dedge_out)])]
         outs[0].start()
         outs[1].start()
 
-        dp_sum(0)
+        with jax.named_scope('dp_sum_0'):
+            dp_sum(0)
 
         def send_rest(j):
             for d in SEND_ORDER:
@@ -636,12 +671,16 @@
                 edge_copy(GRAD_OUT, j, d).wait_recv()
                 place_edges(gedge_raw, de_recv[slot(d), :, at(j, EC)], d, j)
 
-        loop(hold, place_g)
+        with jax.named_scope('place_first'):
+            loop(hold, place_g)
         for l in range(layers):
-            cross_sum(l)
-        loop(nch, place_g, hold)
+            with jax.named_scope(f'cross_sum_{l}'):
+                cross_sum(l)
+        with jax.named_scope('place_rest'):
+            loop(nch, place_g, hold)
         outs[3].start()
-        dn_copy.wait_recv()
+        with jax.named_scope('d_node_wait'):
+            dn_copy.wait_recv()
         gnode_raw[ox] = dn_recv[:, :nodes].astype(BF)
         outs[2].start()
 
@@ -692,6 +731,32 @@
         bf(layers, 2 * D, D), bf(layers, D, 2 * D), bf(layers, D, D), bf(layers, D, D), pltpu.VMEM((D, D), F32))
 
 
+def finish_kernel(*refs):
+    count = (len(refs) - 2) // 3
+    srcs, dsts, bufs, (in_sem, out_sem) = refs[:count], refs[count:2 * count], refs[2 * count:3 * count], refs[3 * count:]
+    pulls = [pltpu.make_async_copy(src, buf, in_sem.at[k]) for k, (src, buf) in enumerate(zip(srcs, bufs))]
+    puts = [pltpu.make_async_copy(buf, dst, out_sem.at[k]) for k, (buf, dst) in enumerate(zip(bufs, dsts))]
+    for pull in pulls:
+        pull.start()
+    for pull, put in zip(pulls, puts):
+        pull.wait()
+        put.start()
+    for put in puts:
+        put.wait()
+
+
+def finish(arrays):
+    sems = pltpu.SemaphoreType.DMA((len(arrays),))
+    return pl.pallas_call(
+        finish_kernel,
+        name='finish',
+        out_shape=[jax.ShapeDtypeStruct(a.shape, a.dtype) for a in arrays],
+        in_specs=[HB] * len(arrays),
+        out_specs=[HB] * len(arrays),
+        scratch_shapes=[pltpu.VMEM(a.shape, a.dtype) for a in arrays] + [sems, sems],
+    )(*arrays)
+
+
 def solution(mesh):
     lat_spec = P('dp', None, 'tp')
     first_spec = P(None, None, 'tp', None)
@@ -712,12 +777,10 @@
         per = SLABS // dpn
         dims = (layers, cols, nodes, edges, npad, eh, dpn)
         flat = lambda arr: jnp.swapaxes(arr, 1, 2)
-        idx = jnp.pad(jnp.stack([senders, receivers]), ((0, 0), (0, 2 * eh - edges)), constant_values=-1).reshape(2, 2 * eh // D, D)
-        vec_in = jnp.concatenate([jnp.transpose(edge_vec, (1, 0, 2)).reshape(-1, cols), jnp.transpose(node_vec, (1, 0, 2)).reshape(-1, cols),
-                                  jnp.zeros((HEAD - 6 * layers, cols), F32)], axis=0)
-        b1_in = jnp.transpose(stacked([edge_b1, node_b1]))
-        args = (flat(node_lat), flat(edge_lat), flat(grad_node), flat(grad_edge), idx,
-                edge_w1.reshape(-1, D), flat(edge_w2).reshape(-1, D), node_w1.reshape(-1, D), flat(node_w2).reshape(-1, D), vec_in, b1_in)
+        lead = lambda arr: jnp.transpose(arr, (1, 0, 2))
+        args = (flat(node_lat), flat(edge_lat), flat(grad_node), flat(grad_edge), senders, receivers,
+                edge_w1.reshape(-1, D), flat(edge_w2).reshape(-1, D), node_w1.reshape(-1, D), flat(node_w2).reshape(-1, D),
+                lead(edge_vec), lead(node_vec), edge_b1, node_b1)
         vm, sem = pltpu.VMEM, pltpu.SemaphoreType.DMA
         wrows = HEAD + layers * LROWS
         lat_n, lat_e = (2, cols, nodes), (2, cols, edges)
@@ -729,7 +792,7 @@
             vm((2 * layers, D, npad), F32), vm((2 * layers, D, npad), F32),
             vm((layers, D, eh), F32), vm((layers, D, eh), F32), vm((8, eh), F32),
             vm((layers, D, npad), F32), vm((layers, D, npad), F32), vm((8, npad), F32),
-            vm((D, npad), F32), vm((D, npad), F32), vm((D, npad), F32), vm((layers, 2, 4 * D, D), F32),
+            vm((D, npad), F32), vm((D, npad), F32), vm((D, npad), F32), vm((8, 2 * eh), jnp.int32), vm((D, D), F32), vm((layers, 2, 4 * D, D), F32),
             vm((layers, SLABS, D, D), F32), vm((layers, 2, SLABS, cols, D), F32), vm((layers, SLABS, 2, cols, D), F32),
             vm((layers, dpn - 1, per, 2, cols, D), F32), vm((layers, per, cols, D), F32), vm((layers, per, cols, D), F32),
             vm((layers, per, cols, D), F32), vm((layers, SLABS, cols, D), F32),
@@ -743,13 +806,13 @@
             lambda *refs: step_kernel(dims, *refs),
             name='graph_step',
             out_shape=outs,
-            in_specs=[HB] * 4 + [VM] * 7,
+            in_specs=[HB] * 4 + [VM] * 10,
             out_specs=[HB] * 4 + [VM] * 8,
             scratch_shapes=scratch,
             compiler_params=pltpu.CompilerParams(collective_id=0, has_side_effects=True, vmem_limit_bytes=67_043_328),
         )(*args)
 
-        lead = lambda arr: jnp.transpose(arr, (1, 0, 2))
+        res = finish(res)
         return (flat(res[0]), flat(res[1]), flat(res[2]), flat(res[3]),
                 res[4], res[5], flat(res[6]), lead(res[7]), res[8], res[9], flat(res[10]), lead(res[11]))
 

time: 196 us -> 182 us (0.929)
  local copies, waits for them, and re-layouts: 15.4 us -> 0 us
  Pallas kernels: 177 us -> 181 us
    unnamed x34 -> x0, local copies, waits for them, and re-layouts: 11.6 us -> none
    pallas_call x0 -> x1, Pallas kernels: none -> 3.46 us  [finish(): pl.pallas_call(finish_kernel, name='finish', out_shape=[jax.ShapeDtypeStr...]
where the time goes in v1:
time: 182 us
  Pallas kernels  181 us (99%)
    pallas_call x1, Pallas kernels, local_step(): pl.pallas_call(lambda *refs: step_kernel(dims, *refs), name='graph_step',...  178 us

profile of v1, /device:TPU:0, one launch (start us, length us, event | category | flops | bytes accessed | tf_op | source)
XLA Modules:
  0.0 181.6 jit_solution(1754188564514417098)
XLA Ops:
  0.6 177.5 %graph_step.1 = (bf16[2,32,1885]{2,1,0:T(8,128)(2,1)}, bf16[2,32,10910]{2,1,0:T(8,128)(2,1)}, bf16[2,32,1885]{2,1,0:T(8,128)(2,1)}, bf16[2,32,10910]{2,1,0:T(8,1...) custom-call(bf16[2,32,1885]{2,1,0:T(8,128)(2,1)} %bitcast.24, ...), custom_call_target="tpu_custom_call" | custom-call | tf_op jit(solution)/shard_map/graph_step/pallas_call | solution.py:805
  178.2 3.5 %finish.1 = (bf16[2,32,1885]{2,1,0:T(8,128)(2,1)}, bf16[2,32,10910]{2,1,0:T(8,128)(2,1)}, bf16[2,32,1885]{2,1,0:T(8,128)(2,1)}, bf16[2,32,10910]{2,1,0:T(8,128)(...) custom-call(bf16[2,32,1885]{2,1,0:T(8,128)(2,1)} %get-tuple-element., ...), custom_call_target="tpu_custom_call" | custom-call | tf_op jit(solution)/shard_map/finish/pallas_call | solution.py:750
